TPU v7x, 128 devices: a whole 4x4x4 slice. The times are simulated.
128 devices in a mesh: rep: 2 (over core), dp: 64 (over x, y, z).
Axes of the slice: x: 4, y: 4, z: 4, core: 2. Of those that a mesh axis runs over, the one named last changes fastest.
Arguments:
- x: bfloat16 [128, 2048, 1280], P(('rep', 'dp')), parts along dimension 0
- dy: bfloat16 [128, 2048, 1280], P(('rep', 'dp')), parts along dimension 0
- w_gate: bfloat16 [2, 1280, 3584], replicated
- w_up: bfloat16 [2, 1280, 3584], replicated
- w_down: bfloat16 [2, 3584, 1280], replicated
- m_w_gate: float32 [2, 1280, 3584], replicated
- m_w_up: float32 [2, 1280, 3584], replicated
- m_w_down: float32 [2, 3584, 1280], replicated
- v_w_gate: float32 [2, 1280, 3584], replicated
- v_w_up: float32 [2, 1280, 3584], replicated
- v_w_down: float32 [2, 3584, 1280], replicated
Outputs:
- output 1: bfloat16 [4, 1280, 3584], P('rep'), parts along dimension 0
- output 2: bfloat16 [4, 1280, 3584], P('rep'), parts along dimension 0
- output 3: bfloat16 [4, 3584, 1280], P('rep'), parts along dimension 0
- output 4: float32 [4, 1280, 3584], P('rep'), parts along dimension 0
- output 5: float32 [4, 1280, 3584], P('rep'), parts along dimension 0
- output 6: float32 [4, 3584, 1280], P('rep'), parts along dimension 0
- output 7: float32 [4, 1280, 3584], P('rep'), parts along dimension 0
- output 8: float32 [4, 1280, 3584], P('rep'), parts along dimension 0
- output 9: float32 [4, 3584, 1280], P('rep'), parts along dimension 0
There are 2 independent parts. A program takes and returns all parts, laid end to end along the dimension named above; an argument that names none is the same for every part.
All inputs are finite; a program needn't handle non-finite values.
Results may differ from a plain program's by a relative error of at most 0.022.
Values are sent between devices in bfloat16 or wider.
A program may use at most 1.5 GiB of HBM per device.

v0:
```python
import jax
import jax.numpy as jnp
from jax import lax
from jax.sharding import PartitionSpec as P

NAMES = ("w_gate", "w_up", "w_down")


def matmul(a, w):
    return jnp.dot(a, w, preferred_element_type=jnp.float32).astype(jnp.bfloat16)


def normed(h):
    wide = h.astype(jnp.float32)
    scale = lax.rsqrt(jnp.mean(wide**2, -1, keepdims=True) + 1e-6)
    return (wide * scale).astype(jnp.bfloat16)


def layer(h, w):
    a = normed(h)
    gate = jnp.dot(a, w["w_gate"], preferred_element_type=jnp.float32)
    up = jnp.dot(a, w["w_up"], preferred_element_type=jnp.float32)
    return h + matmul((jax.nn.silu(gate) * up).astype(jnp.bfloat16), w["w_down"])


def adamw(w, m, v, g):
    m = 0.9 * m + 0.1 * g
    v = 0.95 * v + 0.05 * g * g
    step = m * lax.rsqrt(v + 1e-8) + 0.1 * w
    return (w - 0.02 * step).astype(jnp.bfloat16), m, v


def solution(mesh):
    def step(x, dy, *arrays):
        weights, m, v = (arrays[i : i + 3] for i in (0, 3, 6))
        layers = weights[0].shape[0]
        h, kept = x[0], []
        for number in range(layers):
            kept.append(h)
            h = layer(h, {name: w[number] for name, w in zip(NAMES, weights, strict=True)})
        by_h, summed = dy[0], [None] * layers
        for number in reversed(range(layers)):
            _, back = jax.vjp(lambda w, h: layer(h, w), {name: w[number] for name, w in zip(NAMES, weights, strict=True)}, kept[number])
            by_w, by_h = back(by_h)
            summed[number] = [lax.psum(by_w[name], "dp") for name in NAMES]
        gradients = [jnp.stack([summed[number][i] for number in range(layers)]).astype(jnp.float32) for i in range(3)]
        new = [adamw(w.astype(jnp.float32), m, v, g) for w, m, v, g in zip(weights, m, v, gradients, strict=True)]
        return tuple(one[which] for which in range(3) for one in new)

    return jax.shard_map(
        step,
        mesh=mesh,
        in_specs=(P(("rep", "dp"), None, None),) * 2 + (P(None, None, None),) * 9,
        out_specs=(P("rep", None, None),) * 9,
        check_vma=False,
    )
```

profile of v0, /device:TPU:0, one launch (start us, length us, event | category | flops | bytes accessed | tf_op | source)
XLA Modules:
  0.0 1172.0 jit_solution(1878283186458003980)
XLA Ops:
  7.2 0.0 all-reduce.3.cloned.1.call-start
  7.2 8.0 copy.20
  15.2 3.6 fusion.42
  18.8 0.0 copy-start.3
  18.8 27.2 %fusion.62 = f32[2048,3584]{1,0:T(8,128)} fusion(bf16[2,1280,3584]{2,1,0:T(8,128)(2,1)} %param.13, bf16[1,2048,1280]{2,1,0:T(8,128)(2,1)} %param.11, f32[2048]{0:T(1024)S(1)} %add_rsqrt_fusion), kind=kOutput, calls=%fused_computation.95 | convolution fusion | flops 18798346240 | bytes 43786240 | tf_op jit(solution)/shard_map/dot_general | solution.py:21
  46.0 0.0 copy-done.3
  46.0 35.7 %multiply_convert_fusion.1 = (bf16[2048,3584]{1,0:T(8,128)(2,1)}, f32[2048,3584]{1,0:T(8,128)}) fusion(f32[2048,3584]{1,0:T(8,128)} %fusion.62, bf16[2,1280,3584]{2,1,0:T(8,128)(2,1)} %param.14, bf16[1,2048,1280]{2,1,0:T(8,128)(2,1)} %param.11, f32[2048]{0:T(1024)S(1)} %add_rsqrt_fusion), kind=kOutput, calls=%fused_computation.44 | convolution fusion | flops 18842386432 | bytes 87826432 | tf_op jit(solution)/shard_map/dot_general | solution.py:22
  81.7 27.4 %fusion.46 = (f32[2048]{0:T(1024)S(1)}, bf16[2048,1280]{0,1:T(8,128)(2,1)}) fusion(bf16[2048,3584]{1,0:T(8,128)(2,1)} %get-tuple-element.24, bf16[2,3584,1280]{2,1,0:T(8,128)(2,1)} %param.15, bf16[1,2048,1280]{1,2,0:T(8,128)(2,1)} %copy.20), kind=kOutput, calls=%fused_computation.78 | convolution fusion | flops 18803587072 | bytes 34349056 | tf_op jit(solution)/shard_map/dot_general | solution.py:10
  109.1 0.0 copy-start.1
  109.1 0.6 copy-done.1
  109.7 26.1 %convolution_convert_fusion.4 = bf16[2048,3584]{1,0:T(8,128)(2,1)} fusion(bf16[2,3584,1280]{2,1,0:T(8,128)(2,1)} %param.15, bf16[1,2048,1280]{2,1,0:T(8,128)(2,1)} %param.12), kind=kOutput, calls=%fused_computation.63 | convolution fusion | flops 18797821952 | bytes 29097984 | tf_op jit(solution)/shard_map/transpose(jvp())/dot_general | solution.py:10
  135.7 27.2 %fusion.49 = f32[2048,3584]{1,0:T(8,128)} fusion(bf16[2,1280,3584]{2,1,0:T(8,128)(2,1)} %param.14, bf16[2048,1280]{0,1:T(8,128)(2,1)} %get-tuple-element.27, f32[2048]{0:T(1024)S(1)} %fusion.101), kind=kOutput, calls=%fused_computation.82 | convolution fusion | flops 18798346240 | bytes 43786240 | tf_op jit(solution)/shard_map/jvp()/dot_general | solution.py:22
  163.0 45.3 %fusion.17 = (bf16[2048,3584]{1,0:T(8,128)(2,1)}, f32[2048,3584]{1,0:T(8,128)}) fusion(f32[2048,3584]{1,0:T(8,128)} %fusion.49, bf16[2048,3584]{1,0:T(8,128)(2,1)} %convolution_convert_fusion.4, bf16[2,1280,3584]{2,1,0:T(8,128)(2,1)} %param.13, bf16[2048,1280]{0,1:T(8,128)(2,1)} %get-tuple-element.27, f32[2048]{0:T(1024)S(1)} %fusion.101), kind=kOutput, calls=%fused_computation.35 | convolution fusion | flops 18886426624 | bytes 102506496 | tf_op jit(solution)/shard_map/jvp()/dot_general | solution.py:21
  208.3 26.3 %fusion.38 = bf16[1,1280,3584]{2,1,0:T(8,128)(2,1)} fusion(bf16[2048,3584]{1,0:T(8,128)(2,1)} %get-tuple-element.28, bf16[2048,1280]{0,1:T(8,128)(2,1)} %get-tuple-element.27, f32[2048]{0:T(1024)S(1)} %fusion.101), kind=kOutput, calls=%fused_computation.72 | convolution fusion | flops 18798346240 | bytes 29106176 | tf_op jit(solution)/shard_map/transpose(jvp())/dot_general | solution.py:21
  234.6 25.7 %fusion.76 = bf16[2048,1280]{0,1:T(8,128)(2,1)} fusion(bf16[2048,3584]{1,0:T(8,128)(2,1)} %get-tuple-element.28, bf16[2,1280,3584]{2,1,0:T(8,128)(2,1)} %param.13), kind=kOutput, calls=%fused_computation.107 | convolution fusion | flops 18790481920 | bytes 29097984 | tf_op jit(solution)/shard_map/transpose(jvp())/dot_general | solution.py:21
  260.3 0.0 slice-start.2
  260.3 8.0 copy.21
  268.3 0.0 slice-start.3
  268.3 30.6 %fusion.36 = bf16[1,1280,3584]{2,1,0:T(8,128)(2,1)} fusion(bf16[2048,3584]{1,0:T(8,128)(2,1)} %convolution_convert_fusion.4, bf16[2048,1280]{0,1:T(8,128)(2,1)} %get-tuple-element.27, f32[2048]{0:T(1024)S(1)} %fusion.101, f32[2048,3584]{1,0:T(8,128)} %get-tuple-element.29), kind=kOutput, calls=%fused_computation.70 | convolution fusion | flops 18846973952 | bytes 58466304 | tf_op jit(solution)/shard_map/transpose(jvp())/dot_general | solution.py:22
  299.0 0.0 slice-done.2
  299.0 0.0 slice-done.3
  299.0 29.4 %fusion.34 = bf16[1,3584,1280]{2,1,0:T(8,128)(2,1)} fusion(f32[2048,3584]{1,0:T(8,128)} %fusion.49, bf16[1,2048,1280]{2,1,0:T(8,128)(2,1)S(1)} %bitcast.83, f32[2048,3584]{1,0:T(8,128)} %get-tuple-element.29), kind=kOutput, calls=%fused_computation.68 | convolution fusion | flops 18839109632 | bytes 73138176 | tf_op jit(solution)/shard_map/transpose(jvp())/dot_general | solution.py:10
  328.4 0.0 copy-start.2
  328.4 38.6 %fusion.48 = (f32[2048]{0:T(1024)S(1)}, bf16[2048,1280]{0,1:T(8,128)(2,1)}) fusion(bf16[2048,1280]{0,1:T(8,128)(2,1)} %get-tuple-element.27, bf16[2048,1280]{0,1:T(8,128)(2,1)} %fusion.76, bf16[2,1280,3584]{2,1,0:T(8,128)(2,1)} %param.14, bf16[2048,3584]{1,0:T(8,128)(2,1)} %convolution_convert_fusion.4, f32[2048,3584]{1,0:T(8,128)} %get-tuple-element.29), kind=kOutput, calls=%fused_computation.80 | convolution fusion | flops 18850248704 | bytes 68952064 | tf_op jit(solution)/shard_map/transpose(jvp())/dot_general | solution.py:22
  366.9 0.0 copy-done.2
  367.0 12.4 %fusion.89 = bf16[2048,1280]{0,1:T(8,128)(2,1)} fusion(bf16[2048,1280]{0,1:T(8,128)(2,1)} %get-tuple-element.27, bf16[2048,1280]{0,1:T(8,128)(2,1)} %get-tuple-element.31, bf16[1,2048,1280]{1,2,0:T(8,128)(2,1)} %copy.21, f32[2048]{0:T(1024)S(1)} %multiply_multiply_fusion.3, f32[2048]{0:T(1024)S(1)} %fusion.101), kind=kLoop, calls=%fused_computation.112 | loop fusion | flops 18350080 | bytes 20987904 | tf_op jit(solution)/shard_map/transpose(jvp())/add_any | solution.py:14
  379.3 0.0 copy-start
  379.3 0.0 slice-start
  379.4 26.1 %convolution_convert_fusion.3 = bf16[2048,3584]{1,0:T(8,128)(2,1)} fusion(bf16[2048,1280]{0,1:T(8,128)(2,1)} %fusion.89, bf16[2,3584,1280]{2,1,0:T(8,128)(2,1)} %param.15), kind=kOutput, calls=%fused_computation.62 | convolution fusion | flops 18797821952 | bytes 29097984 | tf_op jit(solution)/shard_map/transpose(jvp())/dot_general | solution.py:10
  405.5 0.0 copy-done
  405.5 0.0 slice-start.1
  405.5 0.0 copy-start.4
  405.5 23.6 %fusion.37 = bf16[1,3584,1280]{2,1,0:T(8,128)(2,1)} fusion(bf16[2048,3584]{1,0:T(8,128)(2,1)} %get-tuple-element.24, bf16[2048,1280]{0,1:T(8,128)(2,1)S(1)} %copy-done), kind=kOutput, calls=%fused_computation.71 | convolution fusion | flops 18795069440 | bytes 29097984 | tf_op jit(solution)/shard_map/transpose(jvp())/dot_general | solution.py:10
  429.1 0.0 slice-done
  429.1 0.0 slice-done.1
  429.2 0.0 copy-done.4
  429.2 29.3 %fusion.35 = bf16[1,1280,3584]{2,1,0:T(8,128)(2,1)} fusion(bf16[2048,3584]{1,0:T(8,128)(2,1)} %convolution_convert_fusion.3, f32[2048,3584]{1,0:T(8,128)} %fusion.62, bf16[1,2048,1280]{1,2,0:T(8,128)(2,1)S(1)} %bitcast.81, f32[2048]{0:T(1024)S(1)} %copy-done.4), kind=kOutput, calls=%fused_computation.69 | convolution fusion | flops 18846973952 | bytes 58466304 | tf_op jit(solution)/shard_map/transpose(jvp())/dot_general | solution.py:22
  458.5 36.6 %fusion.39 = bf16[1,1280,3584]{2,1,0:T(8,128)(2,1)} fusion(f32[2048,3584]{1,0:T(8,128)} %fusion.62, f32[2048,3584]{1,0:T(8,128)} %get-tuple-element.25, bf16[2048,3584]{1,0:T(8,128)(2,1)} %convolution_convert_fusion.3, bf16[1,2048,1280]{1,2,0:T(8,128)(2,1)} %copy.20, f32[2048]{0:T(1024)S(1)} %copy-done.4), kind=kOutput, calls=%fused_computation.73 | convolution fusion | flops 18883674112 | bytes 87826432 | tf_op jit(solution)/shard_map/transpose(jvp())/dot_general | solution.py:21
  495.1 0.0 all-reduce.3.cloned.1.call-update
  495.1 474.4 %all-reduce.3.cloned.1.call-done = (bf16[1,1280,3584]{2,1,0:T(8,128)(2,1)}, bf16[1,1280,3584]{2,1,0:T(8,128)(2,1)}, bf16[1,1280,3584]{2,1,0:T(8,128)(2,1)}, bf16...) async-done(((bf16[1,1280,3584]{2,1,0:T(8,128)(2,1)}, bf16[1,1280,3584]{2,1,0:T(8,128)(2,1)}, ...) | async-done | bytes 55050256 | tf_op jit(solution)/shard_map/psum | solution.py:45
  969.5 67.3 %fusion.10 = (bf16[2,3584,1280]{2,1,0:T(8,128)(2,1)}, f32[2,3584,1280]{2,1,0:T(8,128)}, f32[2,3584,1280]{2,1,0:T(8,128)}) fusion(bf16[2,3584,1280]{2,1,0:T(8,128)(2,1)} %param.15, bf16[1,3584,1280]{2,1,0:T(8,128)(2,1)} %get-tuple-element.13, bf16[1,3584,1280]{2,1,0:T(8,128)(2,1)} %get-tuple-element.14, f32[2,3584,1280]{2,1,0:T(8,128)} %param.21, ...), kind=kLoop, calls=%fused_computation.24 | loop fusion | flops 174325760 | bytes 201850880 | tf_op jit(solution)/shard_map/convert_element_type | solution.py:30
  1036.8 128.1 %fusion.2 = (bf16[2,1280,3584]{2,1,0:T(8,128)(2,1)}, f32[2,1280,3584]{2,1,0:T(8,128)}, f32[2,1280,3584]{2,1,0:T(8,128)}, bf16[2,1280,3584]{2,1,0:T(8,128)(2,1)},...) fusion(bf16[2,1280,3584]{2,1,0:T(8,128)(2,1)} %param.13, bf16[1,1280,3584]{2,1,0:T(8,128)(2,1)} %get-tuple-element.9, ...), kind=kLoop, calls=%fused_computation.16 | loop fusion | flops 348651520 | bytes 403701760 | tf_op jit(solution)/shard_map/convert_element_type | solution.py:30
  (5 shorter events, 0.0 us)
Async XLA Ops:
  7.2 962.3 %all-reduce.3.cloned.1.call-start = ((), (), s32[]{:S(2)}) async-start(), calls=%async_computation | async-start | bytes 110100480 | tf_op jit(solution)/shard_map/psum | solution.py:45
  18.8 27.2 %copy-start.3 = (f32[2048]{0:T(1024)}, f32[2048]{0:T(1024)S(1)}, u32[]{:S(2)}) copy-start(f32[2048]{0:T(1024)S(1)} %add_rsqrt_fusion) | copy-start | bytes 24580
  109.1 0.6 copy-start.1
  260.3 38.7 %slice-start.2 = ((s8[5242880]{0:T(1024)(128)(4,1)}), s8[1048576]{0:T(1024)(128)(4,1)S(1)}, s32[]{:S(2)}) async-start(s8[5242880]{0:T(1024)(128)(4,1)} %bitcast.82), calls=%async_computation.3 | async-start | bytes 2097152
  268.3 30.6 %slice-start.3 = ((s8[5242880]{0:T(1024)(128)(4,1)}), s8[4194304]{0:T(1024)(128)(4,1)S(1)}, s32[]{:S(2)}) async-start(s8[5242880]{0:T(1024)(128)(4,1)} %bitcast.82), calls=%async_computation.4 | async-start | bytes 8388608
  328.4 38.6 %copy-start.2 = (f32[2048]{0:T(1024)S(1)}, f32[2048]{0:T(1024)}, u32[]{:S(2)}) copy-start(f32[2048]{0:T(1024)} %copy-done.1) | copy-start | bytes 24580
  379.3 26.1 %copy-start = (bf16[2048,1280]{0,1:T(8,128)(2,1)S(1)}, bf16[2048,1280]{0,1:T(8,128)(2,1)}, u32[]{:S(2)}) copy-start(bf16[2048,1280]{0,1:T(8,128)(2,1)} %fusion.89) | copy-start | bytes 15728644
  379.3 49.8 %slice-start = ((s8[5242880]{0:T(1024)(128)(4,1)}), s8[4194304]{0:T(1024)(128)(4,1)S(1)}, s32[]{:S(2)}) async-start(s8[5242880]{0:T(1024)(128)(4,1)} %bitcast.80), calls=%async_computation.1 | async-start | bytes 8388608
  405.5 23.7 %slice-start.1 = ((s8[5242880]{0:T(1024)(128)(4,1)}), s8[1048576]{0:T(1024)(128)(4,1)S(1)}, s32[]{:S(2)}) async-start(s8[5242880]{0:T(1024)(128)(4,1)} %bitcast.80), calls=%async_computation.2 | async-start | bytes 2097152
  405.5 23.7 %copy-start.4 = (f32[2048]{0:T(1024)S(1)}, f32[2048]{0:T(1024)}, u32[]{:S(2)}) copy-start(f32[2048]{0:T(1024)} %copy-done.3) | copy-start | bytes 24580
Sparse Core Ops, SparseCore 0:
  495.3 474.1 all-reduce.2
where the time goes:
time: 1180 us; the launch traced here: 1170 us
  waiting for transfers between devices  474 us (40%)
  matrix products  455 us (39%)
  other arithmetic  211 us (18%)
  local copies, waits for them, and re-layouts  16.6 us (1%)
  between operations  14.3 us (1%)
    psum x1, waiting for transfers between devices, step(): summed[number] = [lax.psum(by_w[name], 'dp') for name in NAMES]  474 us
    convert_element_type x2, other arithmetic, adamw(): return ((w - 0.02 * step).astype(jnp.bfloat16), m, v)  195 us
    dot_general x5, matrix products, layer(): up = jnp.dot(a, w['w_up'], preferred_element_type=jnp.float32)  161 us
    dot_general x5, matrix products, layer(): gate = jnp.dot(a, w['w_gate'], preferred_element_type=jnp.float32)  161 us
    dot_general x5, matrix products, matmul(): jnp.dot(a, w, preferred_element_type=jnp.float32).astype(jnp.bfloat16)  133 us
  transfers between devices with their start and end apart: 1, of which 1 were waited for; matrix products, arithmetic and copies ran while one was open for 0% of the time, Pallas kernels for 0%

commit v1 on v0

v1 whole, which is shorter than its diff:
```python
import functools

import jax
import jax.numpy as jnp
from jax import lax
from jax.experimental import pallas as pl
from jax.experimental.pallas import tpu as pltpu
from jax.sharding import PartitionSpec as P

F32, BF16 = jnp.float32, jnp.bfloat16
LANES, TILE, WIDE = 128, 16, 256
C = 512
ROWS = 512
SHARE = 80
VMEM = 67_000_000
AB, ABT, ATB = ((1,), (0,)), ((1,), (1,)), ((0,), (0,))
ANY = pl.BlockSpec(memory_space=pl.ANY)
ONCE = pl.Buffered(buffer_count=1)
TOP, BOTTOM = 1, 0

SIDE = 4
DEVICES = SIDE**3
STRIDES = (SIDE * SIDE, SIDE, 1)
ORDERS = ((0, 1, 2), (1, 2, 0), (2, 0, 1))
MATRICES = range(3)
TO = (1, -1)
LOW, HIGH, EVERY = pl.ds(0, 2), pl.ds(2, 2), slice(None)
HALVES = (LOW, HIGH)


def dot(a, b, dims=AB):
    return lax.dot_general(a, b, (dims, ((), ())), preferred_element_type=F32)


def row_scale(wide):
    return lax.rsqrt(jnp.mean(wide * wide, -1, keepdims=True) + 1e-6)


def normed(h):
    wide = h.astype(F32)
    return (wide * row_scale(wide)).astype(BF16)


def span(i, size):
    return slice(i * size, i * size + size)


def rows_of(i, size):
    return pl.ds(i * size, size)


def vmem(*shape, dtype=BF16):
    return pltpu.VMEM(shape, dtype)


def place_of(me):
    return [me // stride % SIDE for stride in STRIDES]


def near(at, d, by):
    return sum(((a + by) % SIDE if i == d else a) * stride for i, (a, stride) in enumerate(zip(at, STRIDES, strict=True)))


def greet():
    at = place_of(lax.axis_index("dp"))
    for d in range(len(STRIDES)):
        for by in TO:
            pl.semaphore_signal(pltpu.get_barrier_semaphore(), device_id={"dp": near(at, d, by)}, device_id_type=pl.DeviceIdType.MESH)


def meet():
    pl.semaphore_wait(pltpu.get_barrier_semaphore(), len(STRIDES) * len(TO))


def remote(at, sems, index, src, dst, d, by):
    send, recv = sems
    return pltpu.make_async_remote_copy(
        src_ref=src, dst_ref=dst, send_sem=send.at[index], recv_sem=recv.at[index], device_id={"dp": near(at, d, by)}, device_id_type=pl.DeviceIdType.MESH
    )


SEMS = (3, 6, 2)


class Scatter:
    wires = (2.4, 5.0, 0.8, 1.6, 0.3, 0.5)

    def __init__(self, rows, start=0):
        self.rows, self.start = rows, start
        self.cut = -(-rows // (TILE + TILE)) * TILE
        block, line, one = (SIDE, SIDE, rows, LANES), (SIDE, rows, LANES), (rows, LANES)
        shapes = (block,) * 5 + (line,) * 3 + (one,) * 4
        self.n = len(shapes)
        dma = pltpu.SemaphoreType.DMA
        self.scratch = [vmem(*s) for _ in MATRICES for s in shapes] + [dma(SEMS), dma(SEMS), dma((3, 4))]
        self.out_shape = jax.ShapeDtypeStruct((3, rows, LANES), BF16)

    def inputs(self, grads):
        return [g.reshape(SIDE, SIDE, SIDE, -1, LANES) for g in grads]

    def bind(self, grads, out, scratch):
        rows = self.rows
        bufs = [scratch[span(c, self.n)] for c in MATRICES]
        *sems, local = scratch[len(MATRICES) * self.n :]
        at = place_of(lax.axis_index("dp"))
        cuts = (pl.ds(0, self.cut), pl.ds(self.cut, self.rows - self.cut))

        def spot(c, phase, by):
            return (at[ORDERS[c][phase]] + by) % SIDE

        def part(c, i2, i3):
            return (i3, i2) if c == 1 else (i2, i3)

        def of_grad(c, by, rest=(EVERY, EVERY)):
            index = list(rest)
            index.insert(ORDERS[c][0], spot(c, 0, by))
            return grads[c].at[(*index, pl.ds(self.start, rows))]

        def copies(step):
            phase, second = divmod(step, 2)
            made = []
            for c in MATRICES:
                to_right, to_left, own, from_l, from_r, half2, from_l2, from_r2, half3, from_l3, from_r3, _ = bufs[c]
                mine = spot(c, 1, 0)
                if phase == 0:
                    ends = (from_l, from_r) if second else [own.at[part(c, h, EVERY)] for h in HALVES]
                    starts = (to_right, to_left) if second else [of_grad(c, 2, part(c, h, EVERY)) for h in HALVES]
                elif phase == 1:
                    ends = (from_l2, from_r2) if second else [half2.at[h] for h in HALVES]
                    starts = [own.at[part(c, spot(c, 1, by), EVERY) if second else part(c, spot(c, 1, 2), h)] for by, h in zip(TO, HALVES, strict=True)]
                else:
                    ends = (from_l3, from_r3) if second else [half3.at[h] for h in cuts]
                    starts = [own.at[part(c, mine, spot(c, phase, by)) if second else (*part(c, mine, spot(c, phase, 2)), h)] for by, h in zip(TO, cuts, strict=True)]
                for i, (src, dst, by) in enumerate(zip(starts, ends, TO, strict=True)):
                    made.append(remote(at, sems, (c, step, i), src, dst, ORDERS[c][phase], by))
            return made

        def loads(c):
            return [pltpu.make_async_copy(of_grad(c, by), bufs[c][i], local.at[c, i]) for i, by in enumerate(TO)]

        def own_load(c):
            return pltpu.make_async_copy(of_grad(c, 0), bufs[c][2], local.at[c, 2])

        def store(c):
            return pltpu.make_async_copy(bufs[c][-1], out.at[c], local.at[c, 3])

        def wide(ref, *index):
            return ref[index].astype(F32)

        def total(c, *index):
            if len(index) == 2:
                return sum(wide(ref, *part(c, *index)) for ref in bufs[c][2:5])
            return total(c, spot(c, 1, 0), *index) + wide(bufs[c][6], *index) + wide(bufs[c][7], *index)

        def put(c, value, *index):
            bufs[c][2][part(c, *index)] = value.astype(BF16)

        def start(step):
            for copy in copies(step):
                copy.start()

        def arrived(step):
            for copy in copies(step):
                copy.wait_recv()

        def tick0():
            start(0)
            for c in MATRICES:
                for copy in loads(c):
                    copy.start()

        def tick1():
            for c in MATRICES:
                for copy in loads(c):
                    copy.wait()
            arrived(0)
            for c in MATRICES:

                @pl.loop(0, 2 * SIDE)
                def _(i):
                    i2, i3 = i // SIDE, i % SIDE
                    for to, at_end in zip(bufs[c][:2], (part(c, i2, i3), part(c, i2 + 2, i3)), strict=True):
                        to[at_end] = (wide(to, *at_end) + wide(bufs[c][2], *at_end)).astype(BF16)

            start(1)
            for c in MATRICES:
                own_load(c).start()

        def tick2():
            for c in MATRICES:
                own_load(c).wait()
            arrived(1)
            for c in MATRICES:
                far = spot(c, 1, 2)
                pl.loop(0, SIDE)(lambda i: put(c, total(c, far, i), far, i))
            start(2)

        def tick3():
            arrived(2)
            for c in MATRICES:
                right, left = (spot(c, 1, by) for by in TO)
                half = bufs[c][5]

                @pl.loop(0, 2)
                def _(i):
                    put(c, total(c, right, i) + wide(half, i), right, i)
                    put(c, total(c, left, i), left, i)
                    put(c, total(c, right, i + 2), right, i + 2)
                    put(c, total(c, left, i + 2) + wide(half, i + 2), left, i + 2)

            start(3)

        def tick4():
            arrived(3)
            for c in MATRICES:
                put(c, total(c, spot(c, 2, 2)), spot(c, 1, 0), spot(c, 2, 2))
            start(4)

        def tick5():
            arrived(4)
            for c in MATRICES:
                sums = [total(c, spot(c, 2, by)) for by in TO]
                for i, by in enumerate(TO):
                    for j, cut in enumerate(cuts):
                        value = sums[i][cut.start : cut.start + cut.size]
                        if i == j:
                            value = value + wide(bufs[c][8], cut)
                        bufs[c][2][(*part(c, spot(c, 1, 0), spot(c, 2, by)), cut)] = value.astype(BF16)
            start(5)

        def tick6():
            arrived(5)
            for c in MATRICES:
                *_, left, right, done = bufs[c]
                done[...] = (total(c, spot(c, 2, 0)) + wide(left, ...) + wide(right, ...)).astype(BF16)
                store(c).start()
            for step in range(len(self.wires)):
                for copy in copies(step):
                    copy.wait_send()
            for c in MATRICES:
                store(c).wait()

        return tick0, tick1, tick2, tick3, tick4, tick5, tick6


class Exchange:
    def __init__(self, key=None, *moves):
        self.moves = [move for move, _ in moves]
        self.inputs = [move.inputs(arrays) for move, arrays in moves]
        self.in_arrays = sum(self.inputs, [])
        self.in_specs = [ANY] * len(self.in_arrays)
        self.out_specs = [ANY] * len(moves)
        self.out_shapes = [move.out_shape for move in self.moves]
        self.scratch = sum((move.scratch for move in self.moves), [])
        talks = dict(collective_id=key, has_side_effects=True) if moves else {}
        self.params = pltpu.CompilerParams(vmem_limit_bytes=VMEM, **talks)

    def split(self, refs, n_in, n_out):
        a = n_in + len(self.in_arrays)
        b = a + n_out + len(self.moves)
        end = len(refs) - len(self.scratch)
        own = refs[:n_in] + refs[a : a + n_out] + refs[b:end]
        return own, (list(refs[n_in:a]), list(refs[a + n_out : b]), list(refs[end:]))

    def bind(self, refs):
        ins, outs, scratch = refs
        ticks = []
        for move, arrays, out in zip(self.moves, self.inputs, outs, strict=True):
            ticks.append(move.bind(ins[: len(arrays)], out, scratch[: len(move.scratch)]))
            ins, scratch = ins[len(arrays) :], scratch[len(move.scratch) :]
        return ticks

    def plan(self, steps, lengths):
        ends, now = [], 0.0
        for length in lengths * steps:
            now += length
            ends.append(now)
        plans = []
        for move in self.moves:
            others = sum(other.rows for other in self.moves) - move.rows
            units = (move.rows + 0.6 * others) / SHARE
            now, where = ends[0], [0]
            for wire in move.wires:
                now += 3.5 + wire * units
                where.append(min(sum(end < now for end in ends), len(ends) - 1))
            where[-1] = len(ends) - 1
            plans.append(where)
        return plans

    def sites(self, refs, steps, lengths):
        if not self.moves:
            return lambda piece: None
        step = pl.program_id(0)
        pl.when(step == 0)(greet)
        pairs = [pair for ticks, where in zip(self.bind(refs), self.plan(steps, lengths), strict=True) for pair in zip(where, ticks, strict=True)]

        def site(piece):
            if piece == 0:
                pl.when(step == 0)(meet)
            for place, tick in pairs:
                if place % len(lengths) == piece:
                    pl.when(step == place // len(lengths))(tick)

        return site

    def alone(self):
        def body(*refs):
            _, extra = self.split(refs, 0, 0)
            greet()
            meet()
            for ticks in zip(*self.bind(extra), strict=True):
                for tick in ticks:
                    tick()

        return pl.pallas_call(
            body,
            in_specs=self.in_specs,
            out_specs=self.out_specs,
            out_shape=self.out_shapes,
            scratch_shapes=self.scratch,
            compiler_params=self.params,
            cost_estimate=pl.CostEstimate(flops=60_000_000_000, bytes_accessed=20_000_000, transcendentals=0),
            name="exchange",
        )(*self.in_arrays)


def swiglu_back(gate, up, dhid):
    sig = lax.logistic(gate)
    silu = gate * sig
    d = dhid.astype(BF16).astype(F32)
    hid = (silu * up).astype(BF16)
    dup = (d * silu).astype(BF16)
    dgate = (d * up * (sig + silu * (1.0 - sig))).astype(BF16)
    return hid, dgate, dup


def put_gradients(a, dy, hid, dgate, dup, gg, gu, gd, site, piece):
    D = a.shape[1]
    for k in range(D // WIDE):
        value = dot(hid[...], dy[:, span(k, WIDE)], ATB).astype(BF16)
        for i in range(C // TILE):
            for j in range(WIDE // LANES):
                half, tile = divmod(WIDE // LANES * k + j, SHARE // TILE)
                gd[2 * i + half, rows_of(tile, TILE)] = value[span(i, TILE), span(j, LANES)]
    site(piece)
    for k in range(2):
        part = a[:, span(k, D // 2)]
        for out, by in ((gg, dgate), (gu, dup)):
            value = dot(part, by[...], ATB).astype(BF16)
            for i in range(D // 2 // SHARE):
                for j in range(C // LANES):
                    out[(D // 2 // SHARE * k + i) * SIDE + j] = value[span(i, SHARE), span(j, LANES)]
        site(piece + 1 + k)


def top_unit(a, dy, wg, wu, wd, gg, gu, gd, dgate_o, dup_o, hid, site, ready):
    blocks = a.shape[0] // ROWS
    for i in range(blocks):
        ready(i)
        r = rows_of(i, ROWS)
        gate = dot(a[r, :], wg[0])
        up = dot(a[r, :], wu[0])
        dhid = dot(dy[r, :], wd[0], ABT)
        hid[r, :], dgate_o[r, :], dup_o[r, :] = swiglu_back(gate, up, dhid)
        site(i)
    put_gradients(a, dy, hid, dgate_o, dup_o, gg, gu, gd, site, blocks)


def by_rows(source, target, sem):
    return [pltpu.make_async_copy(source.at[r], target.at[r], sem.at[i]) for i in range(target.shape[0] // ROWS) for r in (rows_of(i, ROWS),)]


UNIT = pl.BlockSpec((DEVICES, SHARE, LANES), lambda j: (0, j, 0))


def unit_shapes(count):
    return [jax.ShapeDtypeStruct((DEVICES, SHARE * count, LANES), BF16)] * len(MATRICES)


def top_body(exchange, count, n_chain, *refs):
    own, extra = exchange.split(refs, 5 + n_chain, 5)
    a, dy, wg, wu, wd = own[:5]
    *outs, hid, a_v, dy_v, sem = own[5 + n_chain :]
    step = pl.program_id(0)
    loads = list(zip(by_rows(a, a_v, sem.at[0]), by_rows(dy, dy_v, sem.at[1]), strict=True))

    @pl.when(step == 0)
    def _():
        for pair in loads:
            for copy in pair:
                copy.start()

    def ready(i):
        if i < 2:

            @pl.when(step == 0)
            def _():
                for pair in loads[i:] if i else loads[:1]:
                    for copy in pair:
                        copy.wait()

    site = exchange.sites(extra, count, (2.6, 2.4, 2.4, 2.4, 2.7, 2.7, 2.7))
    top_unit(a_v, dy_v, wg, wu, wd, *outs, hid, site, ready)


def top(a, dy, wg, wu, wd, first, count, so_far, exchange):
    T, D = a.shape
    FF = wg.shape[-1]
    col = pl.BlockSpec((1, D, C), lambda j: (TOP, 0, first + j))
    act = pl.BlockSpec((T, C), lambda j: (0, first + j))
    W = C * count
    return pl.pallas_call(
        functools.partial(top_body, exchange, count, len(so_far)),
        grid=(count,),
        in_specs=[ANY, ANY, col, col, pl.BlockSpec((1, C, D), lambda j: (TOP, first + j, 0))] + [ANY] * len(so_far) + exchange.in_specs,
        input_output_aliases={5 + i: 3 + i for i in range(len(so_far))},
        out_specs=[UNIT] * 3 + [act, act] + exchange.out_specs,
        out_shape=unit_shapes(count) + [jax.ShapeDtypeStruct((T, FF), BF16)] * 2 + exchange.out_shapes,
        scratch_shapes=[vmem(T, C), vmem(T, D), vmem(T, D), pltpu.SemaphoreType.DMA((2, T // ROWS))] + exchange.scratch,
        compiler_params=exchange.params,
        cost_estimate=pl.CostEstimate(flops=12 * T * D * W, bytes_accessed=20_000_000, transcendentals=T * W),
        name=f"top{first}",
    )(a, dy, wg, wu, wd, *so_far, *exchange.in_arrays)


def bottom_body(exchange, count, *refs):
    own, extra = exchange.split(refs, 5, 3)
    a, dy, gate, up, wd, gg, gu, gd, hid, dgate, dup = own
    site = exchange.sites(extra, count, (5.0, 2.9, 2.9, 2.9))
    for i in range(a.shape[0] // ROWS):
        r = rows_of(i, ROWS)
        dhid = dot(dy[r, :], wd[0], ABT)
        hid[r, :], dgate[r, :], dup[r, :] = swiglu_back(gate[0, r, :], up[0, r, :], dhid)
    site(0)
    put_gradients(a, dy, hid, dgate, dup, gg, gu, gd, site, 1)


def bottom(a, dy, gate, up, wd, first, count, exchange):
    T, D = a.shape
    whole = pl.BlockSpec((T, D), lambda j: (0, 0), pipeline_mode=ONCE)
    act = pl.BlockSpec((1, T, C), lambda j: (first + j, 0, 0))
    W = C * count
    return pl.pallas_call(
        functools.partial(bottom_body, exchange, count),
        grid=(count,),
        in_specs=[whole, whole, act, act, pl.BlockSpec((1, C, D), lambda j: (BOTTOM, first + j, 0))] + exchange.in_specs,
        out_specs=[UNIT] * 3 + exchange.out_specs,
        out_shape=unit_shapes(count) + exchange.out_shapes,
        scratch_shapes=[vmem(T, C)] * 3 + exchange.scratch,
        compiler_params=exchange.params,
        cost_estimate=pl.CostEstimate(flops=8 * T * D * W, bytes_accessed=20_000_000, transcendentals=T * W),
        name=f"bottom{first}",
    )(a, dy, gate, up, wd, *exchange.in_arrays)


def through_body(exchange, steps, *refs):
    own, extra = exchange.split(refs, 6, 1)
    h1, dy, wg, wu, dgate, dup, dh_o, wg_v, wu_v, sem = own
    D = h1.shape[1]
    parts = D // WIDE
    step = pl.program_id(0)
    blocks = [rows_of(k, WIDE) for k in range(parts)]
    loads = [[pltpu.make_async_copy(w.at[TOP, n], v.at[n], sem.at[i, k]) for i, (w, v) in enumerate(((wg, wg_v), (wu, wu_v)))] for k, n in enumerate(blocks)]

    @pl.when(step == 0)
    def _():
        for pair in loads:
            for copy in pair:
                copy.start()

    site = exchange.sites(extra, steps, (2.2,) * (parts - 1) + (3.5,))
    for k, n in enumerate(blocks):
        if k <= 2:

            @pl.when(step == 0)
            def _():
                for pair in loads[k:] if k == 2 else loads[k : k + 1]:
                    for copy in pair:
                        copy.wait()

        dh_o[:, n] = dot(dgate[...], wg_v[n, :], ABT).astype(BF16) + dot(dup[...], wu_v[n, :], ABT).astype(BF16)
        if k < parts - 1:
            site(k)
    by_a = dh_o[...].astype(F32)
    wide = h1[...].astype(F32)
    scale = row_scale(wide)
    by_scale = jnp.sum(by_a * wide, -1, keepdims=True)
    by_mean = by_scale * (-scale * scale * scale / D)
    dh_o[...] = dy[...] + (by_a * scale + wide * by_mean).astype(BF16)
    site(parts - 1)


def through(h1, dy, wg, wu, dgate, dup, exchange):
    T, D = h1.shape
    FF = wg.shape[-1]
    act = pl.BlockSpec((ROWS, FF), lambda j: (j, 0))
    state = pl.BlockSpec((ROWS, D), lambda j: (j, 0))
    return pl.pallas_call(
        functools.partial(through_body, exchange, T // ROWS),
        grid=(T // ROWS,),
        in_specs=[state, state, ANY, ANY, act, act] + exchange.in_specs,
        out_specs=[state] + exchange.out_specs,
        out_shape=[jax.ShapeDtypeStruct((T, D), BF16)] + exchange.out_shapes,
        scratch_shapes=[vmem(D, FF)] * 2 + [pltpu.SemaphoreType.DMA((2, D // WIDE))] + exchange.scratch,
        compiler_params=exchange.params,
        cost_estimate=pl.CostEstimate(flops=4 * T * D * FF, bytes_accessed=60_000_000, transcendentals=T),
        name="through",
    )(h1, dy, wg, wu, dgate, dup, *exchange.in_arrays)


def forward_body(steps, x, dy, wg, wu, wd, gate_o, up_o, a0_o, h1_o, a1_o, gg, gu, gd, dgate_o, dup_o, h, a, acc, hid, sem):
    j = pl.program_id(0)
    T, D = h.shape
    blocks = T // ROWS
    load, load_dy, save_h1, save_a1 = (
        by_rows(*pair, sem.at[i]) if i < 2 else [pltpu.make_async_copy(pair[0].at[r], pair[1].at[r], sem.at[i, k]) for k in range(blocks) for r in (rows_of(k, ROWS),)]
        for i, pair in enumerate(((x, h), (dy, h), (h, h1_o), (a, a1_o)))
    )
    save_a0 = pltpu.make_async_copy(a, a0_o, sem.at[4, 0])

    @pl.when(j == 0)
    def _():
        for copy in load:
            copy.start()
        for i in range(blocks):
            load[i].wait()

            @pl.loop(i * ROWS // LANES, (i + 1) * ROWS // LANES)
            def _(k):
                r = rows_of(k, LANES)
                a[r, :] = normed(h[r, :])
                acc[r, :] = jnp.zeros((LANES, D), F32)

        save_a0.start()

    @pl.when(j < steps)
    def _():
        half = T // 2

        @pl.loop(0, 2)
        def _(i):
            r = rows_of(i, half)
            gate = dot(a[r, :], wg[0])
            up = dot(a[r, :], wu[0])
            gate_o[0, r, :] = gate
            up_o[0, r, :] = up
            hid[r, :] = (gate * lax.logistic(gate) * up).astype(BF16)

        @pl.loop(0, 2)
        def _(i):
            r = rows_of(i, half)
            for k in range(D // WIDE):
                n = span(k, WIDE)
                acc[r, n] += dot(hid[r, :], wd[0, :, n])

    @pl.when(j == steps - 1)
    def _():
        save_a0.wait()
        for i in range(blocks):

            @pl.loop(i * ROWS // LANES, (i + 1) * ROWS // LANES)
            def _(k):
                r = rows_of(k, LANES)
                new = h[r, :] + acc[r, :].astype(BF16)
                h[r, :] = new
                a[r, :] = normed(new)

            save_h1[i].start()
            save_a1[i].start()

    @pl.when(j == steps)
    def _():
        for save, load in zip(save_h1, load_dy, strict=True):
            save.wait()
            load.start()
        top_unit(a, h, wg, wu, wd, gg, gu, gd, dgate_o, dup_o, hid, lambda piece: None, lambda i: load_dy[i].wait())
        for copy in save_a1:
            copy.wait()


def forward(x, dy, wg, wu, wd):
    T, D = x.shape
    FF = wg.shape[-1]
    n = FF // C
    col = pl.BlockSpec((1, D, C), lambda j: (j // n, 0, j % n))
    act = pl.BlockSpec((1, T, C), lambda j: (jnp.minimum(j, n - 1), 0, 0))
    unit = pl.BlockSpec((DEVICES, SHARE, LANES), lambda j: (0, 0, 0), pipeline_mode=ONCE)
    back = pl.BlockSpec((T, C), lambda j: (0, 0), pipeline_mode=ONCE)
    return pl.pallas_call(
        functools.partial(forward_body, n),
        grid=(n + 1,),
        in_specs=[ANY, ANY, col, col, pl.BlockSpec((1, C, D), lambda j: (j // n, j % n, 0))],
        out_specs=[act, act, ANY, ANY, ANY, unit, unit, unit, back, back],
        out_shape=[jax.ShapeDtypeStruct((n, T, C), F32)] * 2
        + [jax.ShapeDtypeStruct((T, D), BF16)] * 3
        + unit_shapes(1)
        + [jax.ShapeDtypeStruct((T, FF), BF16)] * 2,
        scratch_shapes=[vmem(T, D), vmem(T, D), vmem(T, D, dtype=F32), vmem(T, C), pltpu.SemaphoreType.DMA((5, T // ROWS))],
        compiler_params=pltpu.CompilerParams(vmem_limit_bytes=VMEM),
        cost_estimate=pl.CostEstimate(flops=6 * T * D * FF, bytes_accessed=100_000_000, transcendentals=T * FF),
        name="forward",
    )(x, dy, wg, wu, wd)


def new_values(w, m, v, g):
    m = 0.9 * m + 0.1 * g
    v = 0.95 * v + 0.05 * g * g
    step = m * lax.rsqrt(v + 1e-8) + 0.1 * w
    return (w - 0.02 * step).astype(BF16), m, v


def adamw_body(*refs):
    g, w, m, v = (refs[span(i, 3)] for i in range(4))
    new = refs[-9:]
    for which in MATRICES:

        def take(rows, cols, grad):
            at = (0, rows, cols)
            done = new_values(w[which][at].astype(F32), m[which][at], v[which][at], grad.astype(F32))
            for out, value in zip(new[which::3], done, strict=True):
                out[at] = value

        _, rows, cols = w[which].shape
        if which < 2:
            for i in range(rows // SHARE):
                for j in range(SIDE):
                    take(rows_of(i, SHARE), rows_of(j, LANES), g[which][i * SIDE + j, 0])
        else:
            for i in range(rows // TILE):
                for j in range(cols // LANES):
                    half, tile = divmod(j, SHARE // TILE)
                    take(rows_of(i, TILE), rows_of(j, LANES), g[which][2 * i + half, 0, rows_of(tile, TILE), :])


def adamw(summed, arrays, layer, first, count, so_far):
    D = arrays[0].shape[1]
    summed = summed.reshape(DEVICES, 3, SHARE * count, LANES)

    def grad(which):
        return pl.BlockSpec((DEVICES // SIDE, 1, SHARE, LANES), lambda i: (i % SIDE, which, i // SIDE, 0))

    wide = pl.BlockSpec((1, D // SIDE, C), lambda i: (layer, i % SIDE, first + i // SIDE))
    tall = pl.BlockSpec((1, C // SIDE, D), lambda i: (layer, first * SIDE + i, 0))
    nine = [wide, wide, tall] * 3
    return pl.pallas_call(
        adamw_body,
        grid=(count * SIDE,),
        in_specs=[grad(which) for which in MATRICES] + nine + [ANY] * len(so_far),
        out_specs=nine,
        out_shape=[jax.ShapeDtypeStruct(a.shape, a.dtype) for a in arrays],
        input_output_aliases={12 + i: i for i in range(len(so_far))},
        compiler_params=pltpu.CompilerParams(vmem_limit_bytes=VMEM),
        cost_estimate=pl.CostEstimate(flops=1_000_000_000 * count, bytes_accessed=66 * D * C * count, transcendentals=3 * D * C * count),
        name=f"adamw{layer}_{first}",
    )(summed, summed, summed, *arrays, *so_far)


def solution(mesh):
    def step(x, dy, *arrays):
        x, dy = x[0], dy[0]
        weights = arrays[:3]
        *gates, wd = weights
        one, three, four = (SHARE * count for count in (1, 3, 4))
        gate0, up0, a0, h1, a1, *out = forward(x, dy, *weights)
        g0, back = out[:3], out[3:]
        *out, s0 = top(a1, dy, *weights, 1, 3, back, Exchange(1, (Scatter(one), g0)))
        g1, back = out[:3], out[3:]
        *out, s1 = top(a1, dy, *weights, 4, 3, back, Exchange(2, (Scatter(three), g1)))
        g2, back = out[:3], out[3:]
        dh1, s2 = through(h1, dy, *gates, *back, Exchange(3, (Scatter(three), g2)))
        g3 = bottom(a0, dh1, gate0, up0, wd, 0, 3, Exchange())
        *g4, s3 = bottom(a0, dh1, gate0, up0, wd, 3, 4, Exchange(4, (Scatter(three), g3)))
        (s4,) = Exchange(5, (Scatter(four), g4)).alone()
        new = ()
        for shard, layer, first, count in ((jnp.concatenate([s0, s1, s2], 1), TOP, 0, 7), (s3, BOTTOM, 0, 3), (s4, BOTTOM, 3, 4)):
            new = adamw(lax.all_gather(shard, "dp", axis=0, tiled=False), arrays, layer, first, count, new)
        return tuple(new)

    whole = P(None, None, None)
    return jax.shard_map(
        step, mesh=mesh, in_specs=(P(("rep", "dp"), None, None),) * 2 + (whole,) * 9, out_specs=(P("rep", None, None),) * 9, check_vma=False
    )
```

time: 1180 us -> 793 us (0.67)
  Pallas kernels: 0 us -> 765 us
  waiting for transfers between devices: 474 us -> 0.11 us
  matrix products: 455 us -> 0 us
  other arithmetic: 211 us -> 1.8 us
  local copies, waits for them, and re-layouts: 16.6 us -> 0 us
    pallas_call x0 -> x10, Pallas kernels: none -> 765 us  [the longest x3 204 us: adamw(): pl.pallas_call(adamw_body, grid=(count * SIDE,), in_specs=[grad(which) fo...]
    psum x1 -> x0, waiting for transfers between devices: 474 us -> none  [step(): summed[number] = [lax.psum(by_w[name], 'dp') for name in NAMES]]
    dot_general x15 -> x0, matrix products: 455 us -> none  [the longest x5 161 us: layer(): up = jnp.dot(a, w['w_up'], preferred_element_type=jnp.float32)]
    convert_element_type x2 -> x0, other arithmetic: 195 us -> none  [adamw(): return ((w - 0.02 * step).astype(jnp.bfloat16), m, v)]
    unnamed x20 -> x0, local copies, waits for them, and re-layouts: 16.6 us -> none
    add_any x1 -> x0, other arithmetic: 12.4 us -> none  [normed(): wide = h.astype(jnp.float32)]
  transfers between devices with their start and end apart: 1 -> 3, of which waited for: 1 -> 0; matrix products, arithmetic and copies ran while one was open for 0% -> 0% of each run, Pallas kernels for 0% -> 50%
where the time goes in v1:
time: 793 us; the launch traced here: 781 us
  Pallas kernels  765 us (96%)
  between operations  14.2 us (2%)
    pallas_call x3, Pallas kernels, adamw(): pl.pallas_call(adamw_body, grid=(count * SIDE,), in_specs=[grad(which) fo...  204 us
    pallas_call x2, Pallas kernels, bottom(): pl.pallas_call(functools.partial(bottom_body, exchange, count), grid=(cou...  156 us
    pallas_call x2, Pallas kernels, top(): pl.pallas_call(functools.partial(top_body, exchange, count, len(so_far)),...  148 us
    pallas_call x1, Pallas kernels, forward(): pl.pallas_call(functools.partial(forward_body, n), grid=(n + 1,), in_spec...  98.5 us
    pallas_call x1, Pallas kernels, alone(): pl.pallas_call(body, in_specs=self.in_specs, out_specs=self.out_specs, ou...  92.2 us
    pallas_call x1, Pallas kernels, through(): pl.pallas_call(functools.partial(through_body, exchange, T // ROWS), grid...  67.2 us
  transfers between devices with their start and end apart: 3, of which 0 were waited for; matrix products, arithmetic and copies ran while one was open for 0% of the time, Pallas kernels for 50%

profile of v1, /device:TPU:0, one launch (start us, length us, event | category | flops | bytes accessed | tf_op | source)
XLA Modules:
  0.0 781.1 jit_solution(3304517009271424206)
XLA Ops:
  7.2 0.0 all-gather.11.cloned.1.call-start
  7.2 98.5 %forward.1 = (f32[7,2048,512]{2,1,0:T(8,128)}, f32[7,2048,512]{2,1,0:T(8,128)}, bf16[2048,1280]{1,0:T(8,128)(2,1)}, bf16[2048,1280]{1,0:T(8,128)(2,1)}, bf16[204...) custom-call(bf16[2048,1280]{1,0:T(8,128)(2,1)} %bitcast.29, ...), custom_call_target="tpu_custom_call" | custom-call | flops 56371445760 | bytes 100000000 | tf_op jit(solution)/shard_map/forward/pallas_call | solution.py:589
  105.7 71.7 %top1.1 = (bf16[64,240,128]{2,1,0:T(8,128)(2,1)}, bf16[64,240,128]{2,1,0:T(8,128)(2,1)}, bf16[64,240,128]{2,1,0:T(8,128)(2,1)}, bf16[2048,3584]{1,0:T(8,128)(2,1...) custom-call(bf16[2048,1280]{1,0:T(8,128)(2,1)} %get-tuple-element.60.ref, ...), custom_call_target="tpu_custom_call", output_to_operand_aliasing={{3}: (5, {}), {4}: (6, {})} | custom-call | flops 48318382080 | bytes 20000000 | tf_op jit(solution)/shard_map/top1/pallas_call | solution.py:412
  177.4 76.0 %top4.1 = (bf16[64,240,128]{2,1,0:T(8,128)(2,1)}, bf16[64,240,128]{2,1,0:T(8,128)(2,1)}, bf16[64,240,128]{2,1,0:T(8,128)(2,1)}, bf16[2048,3584]{1,0:T(8,128)(2,1...) custom-call(bf16[2048,1280]{1,0:T(8,128)(2,1)} %get-tuple-element.60.re, ...), custom_call_target="tpu_custom_call", output_to_operand_aliasing={{3}: (5, {}), {4}: (6, {})} | custom-call | flops 48318382080 | bytes 20000000 | tf_op jit(solution)/shard_map/top4/pallas_call | solution.py:412
  253.4 67.2 %through.1 = (bf16[2048,1280]{1,0:T(8,128)(2,1)}, bf16[3,240,128]{2,1,0:T(8,128)(2,1)}) custom-call(bf16[2048,1280]{1,0:T(8,128)(2,1)} %get-tuple-element.59.refs_0_, bf16[2048,1280]{1,0:T(8,128)(2,1)} %bitcast.33, bf16[2,1280,3584]{2,1,0:T(8,128)(2,1)} %refs_3_.11, bf16[2,1280,3584]{2,1,0:T(8,128)(2,1)} %refs_4_.13, ...), custom_call_target="tpu_custom_call" | custom-call | flops 37580963840 | bytes 60000000 | tf_op jit(solution)/shard_map/through/pallas_call | solution.py:498
  320.6 1.8 pad_maximum_fusion
  322.4 0.0 all-gather.11.cloned.1.call-update
  322.4 0.0 all-gather.9.cloned.1.call-start
  322.5 44.3 %bottom0.1 = (bf16[64,240,128]{2,1,0:T(8,128)(2,1)}, bf16[64,240,128]{2,1,0:T(8,128)(2,1)}, bf16[64,240,128]{2,1,0:T(8,128)(2,1)}) custom-call(bf16[2048,1280]{1,0:T(8,128)(2,1)} %get-tuple-element.58.refs_0_, bf16[2048,1280]{1,0:T(8,128)(2,1)} %get-tuple-element.76.refs_1_, f32[7,2048,512]{2,1,0:T(8,128)} %get-tuple-element.77.refs_2_, ...), custom_call_target="tpu_custom_call" | custom-call | flops 32212254720 | bytes 20000000 | tf_op jit(solution)/shard_map/bottom0/pallas_call | solution.py:443
  366.7 111.5 %bottom3.1 = (bf16[64,320,128]{2,1,0:T(8,128)(2,1)}, bf16[64,320,128]{2,1,0:T(8,128)(2,1)}, bf16[64,320,128]{2,1,0:T(8,128)(2,1)}, bf16[3,240,128]{2,1,0:T(8,128)(2,1)}) custom-call(bf16[2048,1280]{1,0:T(8,128)(2,1)} %get-tuple-element.58.refs_0_, bf16[2048,1280]{1,0:T(8,128)(2,1)} %get-tuple-element.76.refs_1_, f32[7,2048,512]{2,1,0:T(8,128)} %get-tuple-element.77.refs_2_, ...), custom_call_target="tpu_custom_call" | custom-call | flops 42949672960 | bytes 20000000 | tf_op jit(solution)/shard_map/bottom3/pallas_call | solution.py:443
  478.3 0.0 all-gather.9.cloned.1.call-update
  478.3 0.0 all-gather.7.cloned.1.call-start
  478.3 92.2 %exchange.1 = bf16[3,320,128]{2,1,0:T(8,128)(2,1)} custom-call(bf16[4,4,4,320,128]{4,3,2,1,0:T(8,128)(2,1)} %bitcast.34, bf16[4,4,4,320,128]{4,3,2,1,0:T(8,128)(2,1)} %bitcast.35, bf16[4,4,4,320,128]{4,3,2,1,0:T(8,128)(2,1)} %bitcast.36), custom_call_target="tpu_custom_call" | custom-call | flops 60000002048 | bytes 20000000 | tf_op jit(solution)/shard_map/exchange/pallas_call | solution.py:315
  570.5 0.0 all-gather.7.cloned.1.call-update
  570.5 0.0 all-gather.11.cloned.1.call-done
  570.5 101.4 %adamw1_0.1 = (bf16[2,1280,3584]{2,1,0:T(8,128)(2,1)}, bf16[2,1280,3584]{2,1,0:T(8,128)(2,1)}, bf16[2,3584,1280]{2,1,0:T(8,128)(2,1)}, f32[2,1280,3584]{2,1,0:T(...) custom-call(bf16[64,3,560,128]{3,2,1,0:T(8,128)(2,1)} %bitcast.20, ...), custom_call_target="tpu_custom_call" | custom-call | flops 7000000000 | bytes 302776320 | tf_op jit(solution)/shard_map/adamw1_0/pallas_call | solution.py:645
  672.0 0.0 all-gather.9.cloned.1.call-done
  672.0 43.9 %adamw0_0.1 = (bf16[2,1280,3584]{2,1,0:T(8,128)(2,1)}, bf16[2,1280,3584]{2,1,0:T(8,128)(2,1)}, bf16[2,3584,1280]{2,1,0:T(8,128)(2,1)}, f32[2,1280,3584]{2,1,0:T(...) custom-call(bf16[64,3,240,128]{3,2,1,0:T(8,128)(2,1)} %bitcast.26, ...), custom_call_target="tpu_custom_call", output_to_operand_aliasing={{0}: (12, {}), {1}: (13, {}), {2}: (14, {}), {3}: (15, {}),... | custom-call | flops 3000000000 | bytes 129761280 | tf_op jit(solution)/shard_map/adamw0_0/pallas_call | solution.py:645
  715.9 0.0 all-gather.7.cloned.1.call-done
  715.9 58.2 %adamw0_3.1 = (bf16[2,1280,3584]{2,1,0:T(8,128)(2,1)}, bf16[2,1280,3584]{2,1,0:T(8,128)(2,1)}, bf16[2,3584,1280]{2,1,0:T(8,128)(2,1)}, f32[2,1280,3584]{2,1,0:T(...) custom-call(bf16[64,3,320,128]{3,2,1,0:T(8,128)(2,1)} %bitcast.23, ...), custom_call_target="tpu_custom_call", output_to_operand_aliasing={{0}: (12, {}), {1}: (13, {}), {2}: (14, {}), {3}: (15, {}),... | custom-call | flops 4000000000 | bytes 173015040 | tf_op jit(solution)/shard_map/adamw0_3/pallas_call | solution.py:645
Async XLA Ops:
  7.2 563.4 %all-gather.11.cloned.1.call-start = ((), (), s32[]{:S(2)}) async-start(), calls=%async_computation.2 | async-start | bytes 27955200 | tf_op jit(solution)/shard_map/all_gather | solution.py:676
  322.4 349.6 %all-gather.9.cloned.1.call-start = ((), (), s32[]{:S(2)}) async-start(), calls=%async_computation.1 | async-start | bytes 11980800 | tf_op jit(solution)/shard_map/all_gather | solution.py:676
  478.3 237.6 %all-gather.7.cloned.1.call-start = ((), (), s32[]{:S(2)}) async-start(), calls=%async_computation | async-start | bytes 15974400 | tf_op jit(solution)/shard_map/all_gather | solution.py:676
Sparse Core Ops, SparseCore 0:
  322.5 185.7 all-gather.10
  511.2 88.5 all-gather.8
  602.6 99.5 all-gather.6

commit v2 on v1

--- a/solution.py
+++ b/solution.py
@@ -17,6 +17,7 @@
 ANY = pl.BlockSpec(memory_space=pl.ANY)
 ONCE = pl.Buffered(buffer_count=1)
 TOP, BOTTOM = 1, 0
+STEPS = 2
 
 SIDE = 4
 DEVICES = SIDE**3
@@ -83,7 +84,7 @@
 
 
 class Scatter:
-    wires = (2.4, 5.0, 0.8, 1.6, 0.3, 0.5)
+    wires = (2.2, 4.6, 0.7, 1.5, 0.3, 0.5)
 
     def __init__(self, rows, start=0):
         self.rows, self.start = rows, start
@@ -277,11 +278,11 @@
             ends.append(now)
         plans = []
         for move in self.moves:
-            others = sum(other.rows for other in self.moves) - move.rows
-            units = (move.rows + 0.6 * others) / SHARE
+            waits = [3.0 + wire * move.rows / SHARE for wire in move.wires]
+            stretch = min(max((ends[-1] - ends[0]) / sum(waits), 1.0), 1.6)
             now, where = ends[0], [0]
-            for wire in move.wires:
-                now += 3.5 + wire * units
+            for wait in waits:
+                now += wait * stretch
                 where.append(min(sum(end < now for end in ends), len(ends) - 1))
             where[-1] = len(ends) - 1
             plans.append(where)
@@ -637,14 +638,14 @@
     summed = summed.reshape(DEVICES, 3, SHARE * count, LANES)
 
     def grad(which):
-        return pl.BlockSpec((DEVICES // SIDE, 1, SHARE, LANES), lambda i: (i % SIDE, which, i // SIDE, 0))
-
-    wide = pl.BlockSpec((1, D // SIDE, C), lambda i: (layer, i % SIDE, first + i // SIDE))
-    tall = pl.BlockSpec((1, C // SIDE, D), lambda i: (layer, first * SIDE + i, 0))
+        return pl.BlockSpec((DEVICES // STEPS, 1, SHARE, LANES), lambda i: (i % STEPS, which, i // STEPS, 0))
+
+    wide = pl.BlockSpec((1, D // STEPS, C), lambda i: (layer, i % STEPS, first + i // STEPS))
+    tall = pl.BlockSpec((1, C // STEPS, D), lambda i: (layer, first * STEPS + i, 0))
     nine = [wide, wide, tall] * 3
     return pl.pallas_call(
         adamw_body,
-        grid=(count * SIDE,),
+        grid=(count * STEPS,),
         in_specs=[grad(which) for which in MATRICES] + nine + [ANY] * len(so_far),
         out_specs=nine,
         out_shape=[jax.ShapeDtypeStruct(a.shape, a.dtype) for a in arrays],
@@ -671,9 +672,11 @@
         g3 = bottom(a0, dh1, gate0, up0, wd, 0, 3, Exchange())
         *g4, s3 = bottom(a0, dh1, gate0, up0, wd, 3, 4, Exchange(4, (Scatter(three), g3)))
         (s4,) = Exchange(5, (Scatter(four), g4)).alone()
+        parts = [jnp.concatenate([s0, s1, s2], 1), s3, s4]
+        summed = [lax.all_gather(part, "dp", axis=0, tiled=False) for part in parts]
         new = ()
-        for shard, layer, first, count in ((jnp.concatenate([s0, s1, s2], 1), TOP, 0, 7), (s3, BOTTOM, 0, 3), (s4, BOTTOM, 3, 4)):
-            new = adamw(lax.all_gather(shard, "dp", axis=0, tiled=False), arrays, layer, first, count, new)
+        for g, layer, first, count in zip(summed, (TOP, BOTTOM, BOTTOM), (0, 0, 3), (7, 3, 4), strict=True):
+            new = adamw(g, arrays, layer, first, count, new)
         return tuple(new)
 
     whole = P(None, None, None)

time: 793 us -> 780 us (0.984)
  Pallas kernels: 765 us -> 750 us
    pallas_call x3, Pallas kernels: 204 us -> 190 us  [adamw(): pl.pallas_call(adamw_body, grid=(count * STEPS,), in_specs=[grad(which) f...]
where the time goes in v2:
time: 780 us; the launch traced here: 766 us
  Pallas kernels  750 us (96%)
  between operations  14.2 us (2%)
    pallas_call x3, Pallas kernels, adamw(): pl.pallas_call(adamw_body, grid=(count * STEPS,), in_specs=[grad(which) f...  190 us
    pallas_call x2, Pallas kernels, bottom(): pl.pallas_call(functools.partial(bottom_body, exchange, count), grid=(cou...  156 us
    pallas_call x2, Pallas kernels, top(): pl.pallas_call(functools.partial(top_body, exchange, count, len(so_far)),...  145 us
    pallas_call x1, Pallas kernels, forward(): pl.pallas_call(functools.partial(forward_body, n), grid=(n + 1,), in_spec...  98.5 us
    pallas_call x1, Pallas kernels, alone(): pl.pallas_call(body, in_specs=self.in_specs, out_specs=self.out_specs, ou...  90.1 us
    pallas_call x1, Pallas kernels, through(): pl.pallas_call(functools.partial(through_body, exchange, T // ROWS), grid...  69.8 us
  transfers between devices with their start and end apart: 3, of which 0 were waited for; matrix products, arithmetic and copies ran while one was open for 0% of the time, Pallas kernels for 50%

profile of v2, /device:TPU:0, one launch (start us, length us, event | category | flops | bytes accessed | tf_op | source)
XLA Modules:
  0.0 766.3 jit_solution(16568604593060929350)
XLA Ops:
  7.2 0.0 all-gather.11.cloned.1.call-start
  7.2 98.5 %forward.1 = (f32[7,2048,512]{2,1,0:T(8,128)}, f32[7,2048,512]{2,1,0:T(8,128)}, bf16[2048,1280]{1,0:T(8,128)(2,1)}, bf16[2048,1280]{1,0:T(8,128)(2,1)}, bf16[204...) custom-call(bf16[2048,1280]{1,0:T(8,128)(2,1)} %bitcast.29, ...), custom_call_target="tpu_custom_call" | custom-call | flops 56371445760 | bytes 100000000 | tf_op jit(solution)/shard_map/forward/pallas_call | solution.py:590
  105.7 68.7 %top1.1 = (bf16[64,240,128]{2,1,0:T(8,128)(2,1)}, bf16[64,240,128]{2,1,0:T(8,128)(2,1)}, bf16[64,240,128]{2,1,0:T(8,128)(2,1)}, bf16[2048,3584]{1,0:T(8,128)(2,1...) custom-call(bf16[2048,1280]{1,0:T(8,128)(2,1)} %get-tuple-element.60.ref, ...), custom_call_target="tpu_custom_call", output_to_operand_aliasing={{3}: (5, {}), {4}: (6, {})} | custom-call | flops 48318382080 | bytes 20000000 | tf_op jit(solution)/shard_map/top1/pallas_call | solution.py:413
  174.5 76.2 %top4.1 = (bf16[64,240,128]{2,1,0:T(8,128)(2,1)}, bf16[64,240,128]{2,1,0:T(8,128)(2,1)}, bf16[64,240,128]{2,1,0:T(8,128)(2,1)}, bf16[2048,3584]{1,0:T(8,128)(2,1...) custom-call(bf16[2048,1280]{1,0:T(8,128)(2,1)} %get-tuple-element.60.re, ...), custom_call_target="tpu_custom_call", output_to_operand_aliasing={{3}: (5, {}), {4}: (6, {})} | custom-call | flops 48318382080 | bytes 20000000 | tf_op jit(solution)/shard_map/top4/pallas_call | solution.py:413
  250.7 69.8 %through.1 = (bf16[2048,1280]{1,0:T(8,128)(2,1)}, bf16[3,240,128]{2,1,0:T(8,128)(2,1)}) custom-call(bf16[2048,1280]{1,0:T(8,128)(2,1)} %get-tuple-element.59.refs_0_, bf16[2048,1280]{1,0:T(8,128)(2,1)} %bitcast.33, bf16[2,1280,3584]{2,1,0:T(8,128)(2,1)} %refs_3_.11, bf16[2,1280,3584]{2,1,0:T(8,128)(2,1)} %refs_4_.13, ...), custom_call_target="tpu_custom_call" | custom-call | flops 37580963840 | bytes 60000000 | tf_op jit(solution)/shard_map/through/pallas_call | solution.py:499
  320.5 1.8 pad_maximum_fusion
  322.3 0.0 all-gather.11.cloned.1.call-update
  322.3 0.0 all-gather.9.cloned.1.call-start
  322.4 44.7 %bottom0.1 = (bf16[64,240,128]{2,1,0:T(8,128)(2,1)}, bf16[64,240,128]{2,1,0:T(8,128)(2,1)}, bf16[64,240,128]{2,1,0:T(8,128)(2,1)}) custom-call(bf16[2048,1280]{1,0:T(8,128)(2,1)} %get-tuple-element.58.refs_0_, bf16[2048,1280]{1,0:T(8,128)(2,1)} %get-tuple-element.76.refs_1_, f32[7,2048,512]{2,1,0:T(8,128)} %get-tuple-element.77.refs_2_, ...), custom_call_target="tpu_custom_call" | custom-call | flops 32212254720 | bytes 20000000 | tf_op jit(solution)/shard_map/bottom0/pallas_call | solution.py:444
  367.0 111.6 %bottom3.1 = (bf16[64,320,128]{2,1,0:T(8,128)(2,1)}, bf16[64,320,128]{2,1,0:T(8,128)(2,1)}, bf16[64,320,128]{2,1,0:T(8,128)(2,1)}, bf16[3,240,128]{2,1,0:T(8,128)(2,1)}) custom-call(bf16[2048,1280]{1,0:T(8,128)(2,1)} %get-tuple-element.58.refs_0_, bf16[2048,1280]{1,0:T(8,128)(2,1)} %get-tuple-element.76.refs_1_, f32[7,2048,512]{2,1,0:T(8,128)} %get-tuple-element.77.refs_2_, ...), custom_call_target="tpu_custom_call" | custom-call | flops 42949672960 | bytes 20000000 | tf_op jit(solution)/shard_map/bottom3/pallas_call | solution.py:444
  478.6 0.0 all-gather.9.cloned.1.call-update
  478.7 0.0 all-gather.7.cloned.1.call-start
  478.7 90.1 %exchange.1 = bf16[3,320,128]{2,1,0:T(8,128)(2,1)} custom-call(bf16[4,4,4,320,128]{4,3,2,1,0:T(8,128)(2,1)} %bitcast.34, bf16[4,4,4,320,128]{4,3,2,1,0:T(8,128)(2,1)} %bitcast.35, bf16[4,4,4,320,128]{4,3,2,1,0:T(8,128)(2,1)} %bitcast.36), custom_call_target="tpu_custom_call" | custom-call | flops 60000002048 | bytes 20000000 | tf_op jit(solution)/shard_map/exchange/pallas_call | solution.py:316
  568.8 0.0 all-gather.7.cloned.1.call-update
  568.8 0.0 all-gather.11.cloned.1.call-done
  568.9 94.9 %adamw1_0.1 = (bf16[2,1280,3584]{2,1,0:T(8,128)(2,1)}, bf16[2,1280,3584]{2,1,0:T(8,128)(2,1)}, bf16[2,3584,1280]{2,1,0:T(8,128)(2,1)}, f32[2,1280,3584]{2,1,0:T(...) custom-call(bf16[64,3,560,128]{3,2,1,0:T(8,128)(2,1)} %bitcast.20, ...), custom_call_target="tpu_custom_call" | custom-call | flops 7000000000 | bytes 302776320 | tf_op jit(solution)/shard_map/adamw1_0/pallas_call | solution.py:646
  663.8 0.0 all-gather.9.cloned.1.call-done
  663.8 41.0 %adamw0_0.1 = (bf16[2,1280,3584]{2,1,0:T(8,128)(2,1)}, bf16[2,1280,3584]{2,1,0:T(8,128)(2,1)}, bf16[2,3584,1280]{2,1,0:T(8,128)(2,1)}, f32[2,1280,3584]{2,1,0:T(...) custom-call(bf16[64,3,240,128]{3,2,1,0:T(8,128)(2,1)} %bitcast.26, ...), custom_call_target="tpu_custom_call", output_to_operand_aliasing={{0}: (12, {}), {1}: (13, {}), {2}: (14, {}), {3}: (15, {}),... | custom-call | flops 3000000000 | bytes 129761280 | tf_op jit(solution)/shard_map/adamw0_0/pallas_call | solution.py:646
  704.8 0.0 all-gather.7.cloned.1.call-done
  704.8 54.6 %adamw0_3.1 = (bf16[2,1280,3584]{2,1,0:T(8,128)(2,1)}, bf16[2,1280,3584]{2,1,0:T(8,128)(2,1)}, bf16[2,3584,1280]{2,1,0:T(8,128)(2,1)}, f32[2,1280,3584]{2,1,0:T(...) custom-call(bf16[64,3,320,128]{3,2,1,0:T(8,128)(2,1)} %bitcast.23, ...), custom_call_target="tpu_custom_call", output_to_operand_aliasing={{0}: (12, {}), {1}: (13, {}), {2}: (14, {}), {3}: (15, {}),... | custom-call | flops 4000000000 | bytes 173015040 | tf_op jit(solution)/shard_map/adamw0_3/pallas_call | solution.py:646
Async XLA Ops:
  7.2 561.7 %all-gather.11.cloned.1.call-start = ((), (), s32[]{:S(2)}) async-start(), calls=%async_computation.2 | async-start | bytes 27955200 | tf_op jit(solution)/shard_map/all_gather | solution.py:676
  322.3 341.4 %all-gather.9.cloned.1.call-start = ((), (), s32[]{:S(2)}) async-start(), calls=%async_computation.1 | async-start | bytes 11980800 | tf_op jit(solution)/shard_map/all_gather | solution.py:676
  478.7 226.1 %all-gather.7.cloned.1.call-start = ((), (), s32[]{:S(2)}) async-start(), calls=%async_computation | async-start | bytes 15974400 | tf_op jit(solution)/shard_map/all_gather | solution.py:676
Sparse Core Ops, SparseCore 0:
  322.4 185.9 all-gather.10
  511.3 88.6 all-gather.8
  602.8 99.9 all-gather.6
